TPU v7x, 32 devices: a whole 2x2x4 slice. The times are simulated.
32 devices in a mesh: expert: 4 (over y, core), fsdp: 8 (over z, x).
Axes of the slice: x: 2, y: 2, z: 4, core: 2. Of those that a mesh axis runs over, the one named last changes fastest.
Arguments:
- gradients: bfloat16 [8, 3584, 1024], P('expert', 'fsdp'), may hold values from -24 to 24, as said below
- owner: int32 [4, 2], P('expert'), may hold values from 0 to 1, each once within a row
Outputs:
- updates: bfloat16 [8, 3584, 1024], P('expert', 'fsdp')
- slot_rms: float32 [4, 8], P('expert', 'fsdp')
Inputs may be any that keep to these rules, and one draw needn't show every extreme that they name: gradients are values of mean zero and unit variance times a factor per expert between 0.5 and 2 and a factor per expert and row slice between 0.5 and 2, each entry within 24 in magnitude. Each row of owner names every place 0 to 1 exactly once.
All inputs are finite; a program needn't handle non-finite values.
Results may differ from a plain program's by a relative error of at most 0.009.
Values may be sent and summed in bfloat16 or wider, within the bound.
A program may use at most 64 MiB of HBM per device.

v0:
```python
import math
import jax
import jax.numpy as jnp
from jax import lax
from jax.sharding import PartitionSpec as P

ROWS = 3584
COLS = 1024
SHARE = 4
ITERS = 3
coef_a = 3.4445
coef_b = -4.775
coef_c = 2.0315
epsilon = 1e-07


def as_sent(value):
    return jax.tree.map(lambda a: a.astype(jnp.bfloat16) if a.dtype == jnp.float32 else a, value)


def partner_2(value, axis, distance):
    mask = 2**distance
    pairs = [(source, source ^ mask) for source in range(lax.axis_size(axis))]
    return lax.ppermute(value, axis, pairs)


def select_half(stacked, bit_value):
    retained = lax.dynamic_index_in_dim(stacked, bit_value, 0, keepdims=False)
    outgoing = lax.dynamic_index_in_dim(stacked, 1 - bit_value, 0, keepdims=False)
    return (retained, outgoing)


def join_halves(own_block, theirs, bit_value):
    leading = jnp.where(bit_value == 0, own_block, theirs)
    trailing = jnp.where(bit_value == 0, theirs, own_block)
    return jnp.concatenate([leading, trailing], axis=0)


def reduce_gram(current, low_bit, high_bit):
    partial_gram = lax.dot_general(
        current, current, (((0,), (0,)), ((), ())), preferred_element_type=jnp.float32
    )
    rounded = lax.optimization_barrier(partial_gram.astype(jnp.bfloat16))
    columns = rounded.shape[1]
    retained, outgoing = select_half(rounded.reshape(2, columns // 2, columns), low_bit)
    arrived = partner_2(as_sent(outgoing), "fsdp", 0).astype(outgoing.dtype)
    pair_sum = retained.astype(jnp.float32) + arrived.astype(jnp.float32)
    retained_pair, outgoing_pair = select_half(pair_sum.reshape(2, columns // 4, columns), high_bit)
    arrived_pair = partner_2(as_sent(outgoing_pair), "fsdp", 1).astype(outgoing_pair.dtype)
    return (retained_pair + arrived_pair).astype(jnp.bfloat16)


def spread_gram(quarter, low_bit, high_bit):
    incoming = partner_2(quarter, "fsdp", 1)
    half_block = join_halves(quarter, incoming, high_bit)
    partner = partner_2(as_sent(half_block), "fsdp", 0).astype(half_block.dtype)
    return join_halves(half_block, partner, low_bit)


def body(gradients, owner):
    expert_count, local_rows, columns = gradients.shape
    fsdp_index = lax.axis_index("fsdp")
    low_bit = fsdp_index % 2
    high_bit = fsdp_index // 2 % 2
    owner_row = owner[0]
    places = jnp.arange(expert_count, dtype=jnp.int32)
    inverse = jnp.sum(
        jnp.where(owner_row[None, :] == places[:, None], places[None, :], 0), axis=1
    ).astype(jnp.int32)
    expert_sums = jnp.sum(jnp.square(gradients.astype(jnp.float32)), axis=(1, 2))
    totals = lax.psum(expert_sums, "fsdp")
    own_expert = lax.dynamic_index_in_dim(inverse, fsdp_index // SHARE, 0, keepdims=False)
    square_sum = lax.dynamic_index_in_dim(totals, own_expert, 0, keepdims=False)
    ordered = jnp.take(gradients, inverse, axis=0)
    outbound = ordered.reshape(expert_count * SHARE, local_rows // SHARE, columns)
    held = lax.all_to_all(outbound, "fsdp", split_axis=0, concat_axis=1, tiled=True)[0]
    norm_value = jnp.sqrt(square_sum)
    current = (held.astype(jnp.float32) / (norm_value + epsilon)).astype(jnp.bfloat16)
    for iteration in range(ITERS):
        quarter = reduce_gram(current, low_bit, high_bit)
        gram_full = spread_gram(quarter, low_bit, high_bit)
        squared = jnp.dot(gram_full, gram_full, preferred_element_type=jnp.float32)
        poly = (coef_b * gram_full.astype(jnp.float32) + coef_c * squared).astype(jnp.bfloat16)
        current = (
            coef_a * current.astype(jnp.float32)
            + jnp.dot(current, poly, preferred_element_type=jnp.float32)
        ).astype(jnp.bfloat16)
    update = (math.sqrt(ROWS) * current.astype(jnp.float32)).astype(jnp.bfloat16)
    returned = lax.all_to_all(update[None], "fsdp", split_axis=1, concat_axis=0, tiled=True)
    slot_order = returned.reshape(expert_count, local_rows, columns)
    updates = jnp.take(slot_order, owner_row, axis=0)
    slot_rms = (norm_value / math.sqrt(ROWS * COLS)).reshape(1, 1).astype(jnp.float32)
    return (updates, slot_rms)


def solution(mesh):
    placed = (P("expert", "fsdp", None), P("expert", None))
    return jax.shard_map(
        body,
        mesh=mesh,
        in_specs=placed,
        out_specs=(P("expert", "fsdp", None), P("expert", "fsdp")),
        check_vma=False,
    )
```

profile of v0, /device:TPU:0, one launch (start us, length us, event | category | flops | bytes accessed | tf_op | source)
XLA Modules:
  0.0 340.0 jit_solution(16962302694401268506)
XLA Ops:
  0.6 0.8 fusion.16
  1.4 0.7 compare_select_fusion
  2.1 0.7 compare_and_fusion
  2.7 2.2 gather_fusion
  4.9 1.5 broadcast_select_fusion.1
  6.4 7.3 %all-to-all-start = ((bf16[8,112,1024]{2,1,0:T(8,128)(2,1)}), bf16[8,112,1024]{2,1,0:T(8,128)(2,1)S(1)}, u32[]{:S(2)}, u32[]{:S(2)}) async-start(bf16[8,112,1024]{2,1,0:T(8,128)(2,1)} %bitcast.71), calls=%async_computation | async-start | bytes 3670016 | tf_op jit(solution)/shard_map/all_to_all | solution.py:76
  13.7 2.1 multiply_reduce_fusion
  15.7 43.7 %psum.7 = f32[2]{0:T(128)S(1)} all-reduce(f32[2]{0:T(128)S(1)} %multiply_reduce_fusion), channel_id=1, replica_groups=mesh['expert'=4,'fsdp'=8] {'fsdp'}, use_global_device_ids=true, to_apply=%region_2.4 | all-reduce | flops 2 | bytes 16 | tf_op jit(solution)/shard_map/psum | solution.py:71
  59.4 0.6 dynamic_slice.46
  62.0 0.6 dynamic_slice.47
  63.3 0.4 divide_convert_fusion
  63.7 2.4 bitcast_convert_fusion
  66.2 1.3 copy-done
  67.5 5.0 %collective-permute-start = (bf16[512,1024]{1,0:T(8,128)(2,1)S(1)}, bf16[512,1024]{1,0:T(8,128)(2,1)S(1)}, u32[]{:S(2)}, u32[]{:S(2)}) collective-permute-start(bf16[512,1024]{1,0:T(8,128)(2,1)S(1)} %dynamic-slice_bitcast_fusion.2), channel_id=1, source_target_pairs={{0,1},{1,0},{2,3},{3,2},{4,5},{5,4},{6,7},{7,6},{8,9},{9,8},{10,11... | collective-permute-start | bytes 3145736 | tf_op jit(solution)/shard_map/ppermute | solution.py:24
  72.6 19.5 %collective-permute-done = bf16[512,1024]{1,0:T(8,128)(2,1)S(1)} collective-permute-done((bf16[512,1024]{1,0:T(8,128)(2,1)S(1)}, bf16[512,1024]{1,0:T(8,128)(2,1)S(1)}, u32[]{:S(2)}, u32[]{:S(2)}) %collective-permute-start) | collective-permute-done | bytes 1048608 | tf_op jit(solution)/shard_map/ppermute | solution.py:24
  92.0 1.6 convert_add_fusion.2
  93.6 0.1 fusion.13
  93.7 3.4 collective-permute-start.1
  97.1 9.9 %collective-permute-done.1 = bf16[256,1024]{1,0:T(8,128)(2,1)S(1)} collective-permute-done((bf16[256,1024]{1,0:T(8,128)(2,1)S(1)}, bf16[256,1024]{1,0:T(8,128)(2,1)S(1)}, u32[]{:S(2)}, u32[]{:S(2)}) %collective-permute-start.1) | collective-permute-done | bytes 524320 | tf_op jit(solution)/shard_map/ppermute | solution.py:24
  107.0 0.1 fusion.12
  107.1 2.1 collective-permute-start.2
  109.2 7.2 %collective-permute-done.2 = bf16[256,1024]{1,0:T(8,128)(2,1)S(1)} collective-permute-done((bf16[256,1024]{1,0:T(8,128)(2,1)S(1)}, bf16[256,1024]{1,0:T(8,128)(2,1)S(1)}, u32[]{:S(2)}, u32[]{:S(2)}) %collective-permute-start.2) | collective-permute-done | bytes 524320 | tf_op jit(solution)/shard_map/ppermute | solution.py:24
  116.5 2.2 collective-permute-start.3
  118.7 18.2 %collective-permute-done.3 = bf16[512,1024]{1,0:T(8,128)(2,1)S(1)} collective-permute-done((bf16[512,1024]{1,0:T(8,128)(2,1)S(1)}, bf16[512,1024]{1,0:T(8,128)(2,1)S(1)}, u32[]{:S(2)}, u32[]{:S(2)}) %collective-permute-start.3) | collective-permute-done | bytes 1048608 | tf_op jit(solution)/shard_map/ppermute | solution.py:24
  136.8 0.5 broadcast_select_fusion.7
  137.4 2.5 add_convert_fusion.2
  139.9 2.1 add_convert_fusion.5
  141.9 2.4 convolution_convert_fusion.1
  144.4 1.8 collective-permute-start.4
  146.2 17.6 %collective-permute-done.4 = bf16[512,1024]{1,0:T(8,128)(2,1)S(1)} collective-permute-done((bf16[512,1024]{1,0:T(8,128)(2,1)S(1)}, bf16[512,1024]{1,0:T(8,128)(2,1)S(1)}, u32[]{:S(2)}, u32[]{:S(2)}) %collective-permute-start.4) | collective-permute-done | bytes 1048608 | tf_op jit(solution)/shard_map/ppermute | solution.py:24
  163.8 0.4 convert_add_fusion.1
  164.3 1.0 collective-permute-start.5
  165.3 13.1 %collective-permute-done.5 = bf16[256,1024]{1,0:T(8,128)(2,1)S(1)} collective-permute-done((bf16[256,1024]{1,0:T(8,128)(2,1)S(1)}, bf16[256,1024]{1,0:T(8,128)(2,1)S(1)}, u32[]{:S(2)}, u32[]{:S(2)}) %collective-permute-start.5) | collective-permute-done | bytes 524320 | tf_op jit(solution)/shard_map/ppermute | solution.py:24
  178.5 0.2 fusion.11
  178.6 1.5 collective-permute-start.6
  180.1 7.7 %collective-permute-done.6 = bf16[256,1024]{1,0:T(8,128)(2,1)S(1)} collective-permute-done((bf16[256,1024]{1,0:T(8,128)(2,1)S(1)}, bf16[256,1024]{1,0:T(8,128)(2,1)S(1)}, u32[]{:S(2)}, u32[]{:S(2)}) %collective-permute-start.6) | collective-permute-done | bytes 524320 | tf_op jit(solution)/shard_map/ppermute | solution.py:24
  188.0 1.8 collective-permute-start.7
  189.8 14.4 %collective-permute-done.7 = bf16[512,1024]{1,0:T(8,128)(2,1)S(1)} collective-permute-done((bf16[512,1024]{1,0:T(8,128)(2,1)S(1)}, bf16[512,1024]{1,0:T(8,128)(2,1)S(1)}, u32[]{:S(2)}, u32[]{:S(2)}) %collective-permute-start.7) | collective-permute-done | bytes 1048608 | tf_op jit(solution)/shard_map/ppermute | solution.py:24
  204.3 0.6 broadcast_select_fusion.5
  204.9 2.7 add_convert_fusion.1
  207.5 2.1 add_convert_fusion.4
  209.6 2.4 convolution_convert_fusion
  212.1 1.5 collective-permute-start.8
  213.7 13.9 %collective-permute-done.8 = bf16[512,1024]{1,0:T(8,128)(2,1)S(1)} collective-permute-done((bf16[512,1024]{1,0:T(8,128)(2,1)S(1)}, bf16[512,1024]{1,0:T(8,128)(2,1)S(1)}, u32[]{:S(2)}, u32[]{:S(2)}) %collective-permute-start.8) | collective-permute-done | bytes 1048608 | tf_op jit(solution)/shard_map/ppermute | solution.py:24
  227.5 0.4 convert_add_fusion
  228.0 0.7 collective-permute-start.9
  228.7 11.2 %collective-permute-done.9 = bf16[256,1024]{1,0:T(8,128)(2,1)S(1)} collective-permute-done((bf16[256,1024]{1,0:T(8,128)(2,1)S(1)}, bf16[256,1024]{1,0:T(8,128)(2,1)S(1)}, u32[]{:S(2)}, u32[]{:S(2)}) %collective-permute-start.9) | collective-permute-done | bytes 524320 | tf_op jit(solution)/shard_map/ppermute | solution.py:24
  239.9 0.2 fusion.10
  240.0 0.4 collective-permute-start.10
  240.4 8.9 %collective-permute-done.10 = bf16[256,1024]{1,0:T(8,128)(2,1)S(1)} collective-permute-done((bf16[256,1024]{1,0:T(8,128)(2,1)S(1)}, bf16[256,1024]{1,0:T(8,128)(2,1)S(1)}, u32[]{:S(2)}, u32[]{:S(2)}) %collective-permute-start.10) | collective-permute-done | bytes 524320 | tf_op jit(solution)/shard_map/ppermute | solution.py:24
  249.4 1.0 collective-permute-start.11
  250.4 13.9 %collective-permute-done.11 = bf16[512,1024]{1,0:T(8,128)(2,1)S(1)} collective-permute-done((bf16[512,1024]{1,0:T(8,128)(2,1)S(1)}, bf16[512,1024]{1,0:T(8,128)(2,1)S(1)}, u32[]{:S(2)}, u32[]{:S(2)}) %collective-permute-start.11) | collective-permute-done | bytes 1048608 | tf_op jit(solution)/shard_map/ppermute | solution.py:24
  264.3 1.5 broadcast_select_fusion.3
  265.9 7.5 %fusion.9 = bf16[1,896,1024]{2,1,0:T(8,128)(2,1)S(1)} fusion(bf16[896,1024]{1,0:T(8,128)(2,1)} %copy-done.3, bf16[512,1024]{1,0:T(8,128)(2,1)} %get-tuple-element.4, bf16[512,1024]{1,0:T(8,128)(2,1)S(1)} %get-tuple-element.3), kind=kOutput, calls=%fused_computation.26 | convolution fusion | flops 4045537280 | bytes 5767168 | tf_op jit(solution)/shard_map/dot_general | solution.py:86
  273.4 4.8 %copy.9 = bf16[1,896,1024]{2,0,1:T(2,128)(2,1)} copy(bf16[1,896,1024]{2,1,0:T(8,128)(2,1)S(1)} %fusion.9) | data formatting | bytes 3670016 | tf_op jit(solution)/shard_map/broadcast_in_dim | solution.py:89
  278.2 0.5 broadcast.84
  278.7 11.4 %reduce = bf16[896,1024]{1,0:T(8,128)(2,1)S(1)} reduce(bf16[896,1,1024]{2,1,0:T(2,128)(2,1)} %bitcast.69, bf16[]{:T(256)} %broadcast.84), dimensions={1}, to_apply=%bitcast.68.reduce_sub_computation | reduce | bytes 3670018
  290.1 3.7 %reshape.106 = bf16[8,2,57344]{2,1,0:T(2,128)(2,1)} reshape(bf16[896,1024]{1,0:T(8,128)(2,1)S(1)} %reduce) | data formatting | bytes 3670016
  293.8 3.6 %all-to-all-start.1 = ((bf16[8,2,57344]{2,1,0:T(2,128)(2,1)}), bf16[8,2,57344]{2,1,0:T(2,128)(2,1)S(1)}, u32[]{:S(2)}, u32[]{:S(2)}) async-start(bf16[8,2,57344]{2,1,0:T(2,128)(2,1)} %reshape.106), calls=%async_computation.1 | async-start | bytes 3670016 | tf_op jit(solution)/shard_map/all_to_all | solution.py:89
  297.4 29.7 %all-to-all-done.1 = bf16[8,2,57344]{2,1,0:T(2,128)(2,1)S(1)} async-done(((bf16[8,2,57344]{2,1,0:T(2,128)(2,1)}), bf16[8,2,57344]{2,1,0:T(2,128)(2,1)S(1)}, u32[]{:S(2)}, u32[]{:S(2)}) %all-to-all-start.1) | async-done | bytes 1835040 | tf_op jit(solution)/shard_map/all_to_all | solution.py:89
  327.1 4.1 %reshape.107 = bf16[896,1,1024]{2,1,0:T(2,128)(2,1)} reshape(bf16[8,2,57344]{2,1,0:T(2,128)(2,1)S(1)} %all-to-all-done.1) | data formatting | bytes 3670016
  331.2 4.0 %copy.7 = bf16[1,896,1024]{2,1,0:T(8,128)(2,1)} copy(bf16[1,896,1024]{2,0,1:T(2,128)(2,1)} %bitcast.70) | data formatting | bytes 3670016
  335.2 2.2 gather_fusion.1
  337.4 1.5 broadcast_select_fusion
  (21 shorter events, 0.8 us)
Async XLA Ops:
  6.4 56.9 %all-to-all-start = ((bf16[8,112,1024]{2,1,0:T(8,128)(2,1)}), bf16[8,112,1024]{2,1,0:T(8,128)(2,1)S(1)}, u32[]{:S(2)}, u32[]{:S(2)}) async-start(bf16[8,112,1024]{2,1,0:T(8,128)(2,1)} %bitcast.71), calls=%async_computation | async-start | bytes 3670016 | tf_op jit(solution)/shard_map/all_to_all | solution.py:76
  63.7 2.4 copy-start.1
  66.1 1.3 copy-start
  67.5 24.5 %collective-permute-start = (bf16[512,1024]{1,0:T(8,128)(2,1)S(1)}, bf16[512,1024]{1,0:T(8,128)(2,1)S(1)}, u32[]{:S(2)}, u32[]{:S(2)}) collective-permute-start(bf16[512,1024]{1,0:T(8,128)(2,1)S(1)} %dynamic-slice_bitcast_fusion.2), channel_id=1, source_target_pairs={{0,1},{1,0},{2,3},{3,2},{4,5},{5,4},{6,7},{7,6},{8,9},{9,8},{10,11... | collective-permute-start | bytes 3145736 | tf_op jit(solution)/shard_map/ppermute | solution.py:24
  93.7 13.2 %collective-permute-start.1 = (bf16[256,1024]{1,0:T(8,128)(2,1)S(1)}, bf16[256,1024]{1,0:T(8,128)(2,1)S(1)}, u32[]{:S(2)}, u32[]{:S(2)}) collective-permute-start(bf16[256,1024]{1,0:T(8,128)(2,1)S(1)} %fusion.13), channel_id=1, source_target_pairs={{0,2},{1,3},{2,0},{3,1},{4,6},{5,7},{6,4},{7,5},{8,10},{9,11},{10,... | collective-permute-start | bytes 1572872 | tf_op jit(solution)/shard_map/ppermute | solution.py:24
  107.1 9.2 %collective-permute-start.2 = (bf16[256,1024]{1,0:T(8,128)(2,1)S(1)}, bf16[256,1024]{1,0:T(8,128)(2,1)S(1)}, u32[]{:S(2)}, u32[]{:S(2)}) collective-permute-start(bf16[256,1024]{1,0:T(8,128)(2,1)S(1)} %fusion.12), channel_id=1, source_target_pairs={{0,2},{1,3},{2,0},{3,1},{4,6},{5,7},{6,4},{7,5},{8,10},{9,11},{10,... | collective-permute-start | bytes 1572872 | tf_op jit(solution)/shard_map/ppermute | solution.py:24
  116.5 20.3 %collective-permute-start.3 = (bf16[512,1024]{1,0:T(8,128)(2,1)S(1)}, bf16[512,1024]{1,0:T(8,128)(2,1)S(1)}, u32[]{:S(2)}, u32[]{:S(2)}) collective-permute-start(bf16[512,1024]{1,0:T(8,128)(2,1)S(1)} %pad_maximum_fusion), channel_id=1, source_target_pairs={{0,1},{1,0},{2,3},{3,2},{4,5},{5,4},{6,7},{7,6},{8,9},{9,8},{10,11... | collective-permute-start | bytes 3145736 | tf_op jit(solution)/shard_map/ppermute | solution.py:24
  137.4 2.5 copy-start.2
  144.4 19.4 %collective-permute-start.4 = (bf16[512,1024]{1,0:T(8,128)(2,1)S(1)}, bf16[512,1024]{1,0:T(8,128)(2,1)S(1)}, u32[]{:S(2)}, u32[]{:S(2)}) collective-permute-start(bf16[512,1024]{1,0:T(8,128)(2,1)S(1)} %dynamic-slice_bitcast_fusion.1), channel_id=1, source_target_pairs={{0,1},{1,0},{2,3},{3,2},{4,5},{5,4},{6,7},{7,6},{8,9},{9,8},{10,11... | collective-permute-start | bytes 3145736 | tf_op jit(solution)/shard_map/ppermute | solution.py:24
  164.3 14.1 %collective-permute-start.5 = (bf16[256,1024]{1,0:T(8,128)(2,1)S(1)}, bf16[256,1024]{1,0:T(8,128)(2,1)S(1)}, u32[]{:S(2)}, u32[]{:S(2)}) collective-permute-start(bf16[256,1024]{1,0:T(8,128)(2,1)S(1)} %fusion.14), channel_id=1, source_target_pairs={{0,2},{1,3},{2,0},{3,1},{4,6},{5,7},{6,4},{7,5},{8,10},{9,11},{10,... | collective-permute-start | bytes 1572872 | tf_op jit(solution)/shard_map/ppermute | solution.py:24
  178.6 9.2 %collective-permute-start.6 = (bf16[256,1024]{1,0:T(8,128)(2,1)S(1)}, bf16[256,1024]{1,0:T(8,128)(2,1)S(1)}, u32[]{:S(2)}, u32[]{:S(2)}) collective-permute-start(bf16[256,1024]{1,0:T(8,128)(2,1)S(1)} %fusion.11), channel_id=1, source_target_pairs={{0,2},{1,3},{2,0},{3,1},{4,6},{5,7},{6,4},{7,5},{8,10},{9,11},{10,... | collective-permute-start | bytes 1572872 | tf_op jit(solution)/shard_map/ppermute | solution.py:24
  188.0 16.3 %collective-permute-start.7 = (bf16[512,1024]{1,0:T(8,128)(2,1)S(1)}, bf16[512,1024]{1,0:T(8,128)(2,1)S(1)}, u32[]{:S(2)}, u32[]{:S(2)}) collective-permute-start(bf16[512,1024]{1,0:T(8,128)(2,1)S(1)} %pad_maximum_fusion.1), channel_id=1, source_target_pairs={{0,1},{1,0},{2,3},{3,2},{4,5},{5,4},{6,7},{7,6},{8,9},{9,8},{10,11... | collective-permute-start | bytes 3145736 | tf_op jit(solution)/shard_map/ppermute | solution.py:24
  209.6 2.4 copy-start.3
  212.1 15.4 %collective-permute-start.8 = (bf16[512,1024]{1,0:T(8,128)(2,1)S(1)}, bf16[512,1024]{1,0:T(8,128)(2,1)S(1)}, u32[]{:S(2)}, u32[]{:S(2)}) collective-permute-start(bf16[512,1024]{1,0:T(8,128)(2,1)S(1)} %dynamic-slice_bitcast_fusion), channel_id=1, source_target_pairs={{0,1},{1,0},{2,3},{3,2},{4,5},{5,4},{6,7},{7,6},{8,9},{9,8},{10,11... | collective-permute-start | bytes 3145736 | tf_op jit(solution)/shard_map/ppermute | solution.py:24
  228.0 11.9 %collective-permute-start.9 = (bf16[256,1024]{1,0:T(8,128)(2,1)S(1)}, bf16[256,1024]{1,0:T(8,128)(2,1)S(1)}, u32[]{:S(2)}, u32[]{:S(2)}) collective-permute-start(bf16[256,1024]{1,0:T(8,128)(2,1)S(1)} %fusion.15), channel_id=1, source_target_pairs={{0,2},{1,3},{2,0},{3,1},{4,6},{5,7},{6,4},{7,5},{8,10},{9,11},{10,... | collective-permute-start | bytes 1572872 | tf_op jit(solution)/shard_map/ppermute | solution.py:24
  240.0 9.2 %collective-permute-start.10 = (bf16[256,1024]{1,0:T(8,128)(2,1)S(1)}, bf16[256,1024]{1,0:T(8,128)(2,1)S(1)}, u32[]{:S(2)}, u32[]{:S(2)}) collective-permute-start(bf16[256,1024]{1,0:T(8,128)(2,1)S(1)} %fusion.10), channel_id=1, source_target_pairs={{0,2},{1,3},{2,0},{3,1},{4,6},{5,7},{6,4},{7,5},{8,10},{9,11},{10,... | collective-permute-start | bytes 1572872 | tf_op jit(solution)/shard_map/ppermute | solution.py:24
  249.4 14.9 %collective-permute-start.11 = (bf16[512,1024]{1,0:T(8,128)(2,1)S(1)}, bf16[512,1024]{1,0:T(8,128)(2,1)S(1)}, u32[]{:S(2)}, u32[]{:S(2)}) collective-permute-start(bf16[512,1024]{1,0:T(8,128)(2,1)S(1)} %pad_maximum_fusion.2), channel_id=1, source_target_pairs={{0,1},{1,0},{2,3},{3,2},{4,5},{5,4},{6,7},{7,6},{8,9},{9,8},{10,11... | collective-permute-start | bytes 3145736 | tf_op jit(solution)/shard_map/ppermute | solution.py:24
  293.8 33.3 %all-to-all-start.1 = ((bf16[8,2,57344]{2,1,0:T(2,128)(2,1)}), bf16[8,2,57344]{2,1,0:T(2,128)(2,1)S(1)}, u32[]{:S(2)}, u32[]{:S(2)}) async-start(bf16[8,2,57344]{2,1,0:T(2,128)(2,1)} %reshape.106), calls=%async_computation.1 | async-start | bytes 3670016 | tf_op jit(solution)/shard_map/all_to_all | solution.py:89
where the time goes:
time: 341 us; the launch traced here: 340 us
  waiting for transfers between devices  185 us (54%)
  blocking collectives  43.7 us (13%)
  starting transfers between devices  33.2 us (10%)
  other arithmetic  24.9 us (7%)
  local copies, waits for them, and re-layouts  24.4 us (7%)
  matrix products  24 us (7%)
  between operations  4.74 us (1%)
    ppermute x12, waiting for transfers between devices, partner_2(): return lax.ppermute(value, axis, pairs)  155 us
    psum x1, blocking collectives, body(): totals = lax.psum(expert_sums, 'fsdp')  43.7 us
    all_to_all x1, waiting for transfers between devices, body(): lax.all_to_all(update[None], 'fsdp', split_axis=1, concat_axis=0, tiled=T...  29.7 us
    ppermute x12, starting transfers between devices, partner_2(): return lax.ppermute(value, axis, pairs)  22.3 us
    unnamed x12, local copies, waits for them, and re-layouts  13.6 us
    dot_general x3, matrix products, body(): jnp.dot(current, poly, preferred_element_type=jnp.float32)  11.7 us
    unnamed x1, other arithmetic  11.4 us
    all_to_all x1, starting transfers between devices, body(): lax.all_to_all(outbound, 'fsdp', split_axis=0, concat_axis=1, tiled=True)[0]  7.28 us
  transfers between devices with their start and end apart: 14, of which 13 were waited for; matrix products, arithmetic and copies ran while one was open for 1% of the time, Pallas kernels for 0%

commit v1 on v0

--- a/solution.py
+++ b/solution.py
@@ -86,7 +86,15 @@
             + jnp.dot(current, poly, preferred_element_type=jnp.float32)
         ).astype(jnp.bfloat16)
     update = (math.sqrt(ROWS) * current.astype(jnp.float32)).astype(jnp.bfloat16)
-    returned = lax.all_to_all(update[None], "fsdp", split_axis=1, concat_axis=0, tiled=True)
+    returned = jnp.concatenate(
+        lax.all_to_all(
+            jnp.stack(jnp.split(update[None], lax.axis_size("fsdp"), axis=1)),
+            axis_name="fsdp",
+            split_axis=0,
+            concat_axis=0,
+        ),
+        axis=0,
+    )
     slot_order = returned.reshape(expert_count, local_rows, columns)
     updates = jnp.take(slot_order, owner_row, axis=0)
     slot_rms = (norm_value / math.sqrt(ROWS * COLS)).reshape(1, 1).astype(jnp.float32)

time: 341 us -> 318 us (0.933)
  local copies, waits for them, and re-layouts: 24.4 us -> 12.7 us
  other arithmetic: 24.9 us -> 13.7 us
    unnamed x1 -> x0, other arithmetic: 11.4 us -> none
    unnamed x12 -> x17, local copies, waits for them, and re-layouts: 13.6 us -> 6.28 us
    broadcast_in_dim x1 -> x0, local copies, waits for them, and re-layouts: 4.84 us -> none  [body(): update[None]]
where the time goes in v1:
time: 318 us; the launch traced here: 317 us
  waiting for transfers between devices  185 us (58%)
  blocking collectives  43.7 us (14%)
  starting transfers between devices  33.2 us (10%)
  matrix products  24.2 us (8%)
  other arithmetic  13.7 us (4%)
  local copies, waits for them, and re-layouts  12.7 us (4%)
  between operations  4.76 us (1%)
    ppermute x12, waiting for transfers between devices, partner_2(): return lax.ppermute(value, axis, pairs)  155 us
    psum x1, blocking collectives, body(): totals = lax.psum(expert_sums, 'fsdp')  43.7 us
    all_to_all x1, waiting for transfers between devices, body(): lax.all_to_all(jnp.stack(jnp.split(update[None], lax.axis_size('fsdp'), a...  29.7 us
    ppermute x12, starting transfers between devices, partner_2(): return lax.ppermute(value, axis, pairs)  22.4 us
    dot_general x3, matrix products, body(): jnp.dot(current, poly, preferred_element_type=jnp.float32)  11.8 us
    all_to_all x1, starting transfers between devices, body(): lax.all_to_all(outbound, 'fsdp', split_axis=0, concat_axis=1, tiled=True)[0]  7.28 us
    dot_general x3, matrix products, reduce_gram(): lax.dot_general(current, current, (((0,), (0,)), ((), ())), preferred_ele...  7.18 us
  transfers between devices with their start and end apart: 14, of which 13 were waited for; matrix products, arithmetic and copies ran while one was open for 1% of the time, Pallas kernels for 0%

profile of v1, /device:TPU:0, one launch (start us, length us, event | category | flops | bytes accessed | tf_op | source)
XLA Modules:
  0.0 317.1 jit_solution(306512624130062416)
XLA Ops:
  0.6 0.8 fusion.24
  1.4 2.2 gather_fusion
  3.6 1.5 broadcast_select_fusion.1
  5.1 7.3 %all-to-all-start = ((bf16[8,112,1024]{2,1,0:T(8,128)(2,1)}), bf16[8,112,1024]{2,1,0:T(8,128)(2,1)S(1)}, u32[]{:S(2)}, u32[]{:S(2)}) async-start(bf16[8,112,1024]{2,1,0:T(8,128)(2,1)} %bitcast.97), calls=%async_computation | async-start | bytes 3670016 | tf_op jit(solution)/shard_map/all_to_all | solution.py:76
  12.4 2.1 multiply_reduce_fusion
  14.4 43.7 %psum.7 = f32[2]{0:T(128)S(1)} all-reduce(f32[2]{0:T(128)S(1)} %multiply_reduce_fusion), channel_id=1, replica_groups=mesh['expert'=4,'fsdp'=8] {'fsdp'}, use_global_device_ids=true, to_apply=%region_2.4 | all-reduce | flops 2 | bytes 16 | tf_op jit(solution)/shard_map/psum | solution.py:71
  58.1 0.6 dynamic_slice.46
  60.7 0.6 dynamic_slice.47
  62.0 0.4 divide_convert_fusion
  62.4 2.4 bitcast_convert_fusion
  64.8 1.3 copy-done
  66.3 5.0 %collective-permute-start = (bf16[512,1024]{1,0:T(8,128)(2,1)S(1)}, bf16[512,1024]{1,0:T(8,128)(2,1)S(1)}, u32[]{:S(2)}, u32[]{:S(2)}) collective-permute-start(bf16[512,1024]{1,0:T(8,128)(2,1)S(1)} %dynamic-slice_bitcast_fusion.2), channel_id=1, source_target_pairs={{0,1},{1,0},{2,3},{3,2},{4,5},{5,4},{6,7},{7,6},{8,9},{9,8},{10,11... | collective-permute-start | bytes 3145736 | tf_op jit(solution)/shard_map/ppermute | solution.py:24
  71.3 19.5 %collective-permute-done = bf16[512,1024]{1,0:T(8,128)(2,1)S(1)} collective-permute-done((bf16[512,1024]{1,0:T(8,128)(2,1)S(1)}, bf16[512,1024]{1,0:T(8,128)(2,1)S(1)}, u32[]{:S(2)}, u32[]{:S(2)}) %collective-permute-start) | collective-permute-done | bytes 1048608 | tf_op jit(solution)/shard_map/ppermute | solution.py:24
  90.7 1.6 convert_add_fusion.2
  92.3 0.1 fusion.13
  92.4 3.4 %collective-permute-start.1 = (bf16[256,1024]{1,0:T(8,128)(2,1)S(1)}, bf16[256,1024]{1,0:T(8,128)(2,1)S(1)}, u32[]{:S(2)}, u32[]{:S(2)}) collective-permute-start(bf16[256,1024]{1,0:T(8,128)(2,1)S(1)} %fusion.13), channel_id=1, source_target_pairs={{0,2},{1,3},{2,0},{3,1},{4,6},{5,7},{6,4},{7,5},{8,10},{9,11},{10,... | collective-permute-start | bytes 1572872 | tf_op jit(solution)/shard_map/ppermute | solution.py:24
  95.8 9.9 %collective-permute-done.1 = bf16[256,1024]{1,0:T(8,128)(2,1)S(1)} collective-permute-done((bf16[256,1024]{1,0:T(8,128)(2,1)S(1)}, bf16[256,1024]{1,0:T(8,128)(2,1)S(1)}, u32[]{:S(2)}, u32[]{:S(2)}) %collective-permute-start.1) | collective-permute-done | bytes 524320 | tf_op jit(solution)/shard_map/ppermute | solution.py:24
  105.7 0.1 fusion.12
  105.8 2.1 collective-permute-start.2
  107.9 7.2 %collective-permute-done.2 = bf16[256,1024]{1,0:T(8,128)(2,1)S(1)} collective-permute-done((bf16[256,1024]{1,0:T(8,128)(2,1)S(1)}, bf16[256,1024]{1,0:T(8,128)(2,1)S(1)}, u32[]{:S(2)}, u32[]{:S(2)}) %collective-permute-start.2) | collective-permute-done | bytes 524320 | tf_op jit(solution)/shard_map/ppermute | solution.py:24
  115.2 2.1 collective-permute-start.3
  117.4 18.2 %collective-permute-done.3 = bf16[512,1024]{1,0:T(8,128)(2,1)S(1)} collective-permute-done((bf16[512,1024]{1,0:T(8,128)(2,1)S(1)}, bf16[512,1024]{1,0:T(8,128)(2,1)S(1)}, u32[]{:S(2)}, u32[]{:S(2)}) %collective-permute-start.3) | collective-permute-done | bytes 1048608 | tf_op jit(solution)/shard_map/ppermute | solution.py:24
  135.5 0.5 broadcast_select_fusion.7
  136.1 2.5 add_convert_fusion.2
  138.6 2.1 add_convert_fusion.5
  140.6 2.4 convolution_convert_fusion.1
  143.1 1.8 collective-permute-start.4
  144.9 17.6 %collective-permute-done.4 = bf16[512,1024]{1,0:T(8,128)(2,1)S(1)} collective-permute-done((bf16[512,1024]{1,0:T(8,128)(2,1)S(1)}, bf16[512,1024]{1,0:T(8,128)(2,1)S(1)}, u32[]{:S(2)}, u32[]{:S(2)}) %collective-permute-start.4) | collective-permute-done | bytes 1048608 | tf_op jit(solution)/shard_map/ppermute | solution.py:24
  162.5 0.4 convert_add_fusion.1
  163.0 1.0 collective-permute-start.5
  164.0 13.1 %collective-permute-done.5 = bf16[256,1024]{1,0:T(8,128)(2,1)S(1)} collective-permute-done((bf16[256,1024]{1,0:T(8,128)(2,1)S(1)}, bf16[256,1024]{1,0:T(8,128)(2,1)S(1)}, u32[]{:S(2)}, u32[]{:S(2)}) %collective-permute-start.5) | collective-permute-done | bytes 524320 | tf_op jit(solution)/shard_map/ppermute | solution.py:24
  177.2 0.2 fusion.11
  177.3 1.5 collective-permute-start.6
  178.9 7.7 %collective-permute-done.6 = bf16[256,1024]{1,0:T(8,128)(2,1)S(1)} collective-permute-done((bf16[256,1024]{1,0:T(8,128)(2,1)S(1)}, bf16[256,1024]{1,0:T(8,128)(2,1)S(1)}, u32[]{:S(2)}, u32[]{:S(2)}) %collective-permute-start.6) | collective-permute-done | bytes 524320 | tf_op jit(solution)/shard_map/ppermute | solution.py:24
  186.7 1.8 collective-permute-start.7
  188.5 14.4 %collective-permute-done.7 = bf16[512,1024]{1,0:T(8,128)(2,1)S(1)} collective-permute-done((bf16[512,1024]{1,0:T(8,128)(2,1)S(1)}, bf16[512,1024]{1,0:T(8,128)(2,1)S(1)}, u32[]{:S(2)}, u32[]{:S(2)}) %collective-permute-start.7) | collective-permute-done | bytes 1048608 | tf_op jit(solution)/shard_map/ppermute | solution.py:24
  203.0 0.6 broadcast_select_fusion.5
  203.5 2.7 add_convert_fusion.1
  206.2 2.1 add_convert_fusion.4
  208.3 2.4 convolution_convert_fusion
  210.8 1.5 collective-permute-start.8
  212.3 13.9 %collective-permute-done.8 = bf16[512,1024]{1,0:T(8,128)(2,1)S(1)} collective-permute-done((bf16[512,1024]{1,0:T(8,128)(2,1)S(1)}, bf16[512,1024]{1,0:T(8,128)(2,1)S(1)}, u32[]{:S(2)}, u32[]{:S(2)}) %collective-permute-start.8) | collective-permute-done | bytes 1048608 | tf_op jit(solution)/shard_map/ppermute | solution.py:24
  226.2 0.4 convert_add_fusion
  226.7 0.7 collective-permute-start.9
  227.4 11.1 %collective-permute-done.9 = bf16[256,1024]{1,0:T(8,128)(2,1)S(1)} collective-permute-done((bf16[256,1024]{1,0:T(8,128)(2,1)S(1)}, bf16[256,1024]{1,0:T(8,128)(2,1)S(1)}, u32[]{:S(2)}, u32[]{:S(2)}) %collective-permute-start.9) | collective-permute-done | bytes 524320 | tf_op jit(solution)/shard_map/ppermute | solution.py:24
  238.5 0.2 fusion.10
  238.7 0.4 collective-permute-start.10
  239.1 8.9 %collective-permute-done.10 = bf16[256,1024]{1,0:T(8,128)(2,1)S(1)} collective-permute-done((bf16[256,1024]{1,0:T(8,128)(2,1)S(1)}, bf16[256,1024]{1,0:T(8,128)(2,1)S(1)}, u32[]{:S(2)}, u32[]{:S(2)}) %collective-permute-start.10) | collective-permute-done | bytes 524320 | tf_op jit(solution)/shard_map/ppermute | solution.py:24
  248.1 1.0 collective-permute-start.11
  249.1 13.9 %collective-permute-done.11 = bf16[512,1024]{1,0:T(8,128)(2,1)S(1)} collective-permute-done((bf16[512,1024]{1,0:T(8,128)(2,1)S(1)}, bf16[512,1024]{1,0:T(8,128)(2,1)S(1)}, u32[]{:S(2)}, u32[]{:S(2)}) %collective-permute-start.11) | collective-permute-done | bytes 1048608 | tf_op jit(solution)/shard_map/ppermute | solution.py:24
  263.0 1.6 broadcast_select_fusion.3
  264.5 7.7 %fusion.9 = bf16[1,896,1024]{2,1,0:T(8,128)(2,1)S(1)} fusion(bf16[896,1024]{1,0:T(8,128)(2,1)} %copy-done.4, bf16[512,1024]{1,0:T(8,128)(2,1)} %get-tuple-element.4, bf16[512,1024]{1,0:T(8,128)(2,1)S(1)} %get-tuple-element.3), kind=kOutput, calls=%fused_computation.26 | convolution fusion | flops 4045537280 | bytes 5767168 | tf_op jit(solution)/shard_map/dot_general | solution.py:86
  272.2 0.7 fusion.23
  272.9 0.7 fusion.22
  273.6 0.7 fusion.21
  274.3 0.7 fusion.20
  275.0 0.7 fusion.19
  275.7 0.7 fusion.18
  276.4 0.7 fusion.17
  277.1 0.7 fusion.16
  277.8 3.6 %all-to-all-start.1 = ((bf16[8,1,112,1024]{3,2,1,0:T(8,128)(2,1)}), bf16[8,1,112,1024]{3,2,1,0:T(8,128)(2,1)S(1)}, u32[]{:S(2)}, u32[]{:S(2)}) async-start(bf16[8,1,112,1024]{3,2,1,0:T(8,128)(2,1)} %fusion.16), calls=%async_computation.1 | async-start | bytes 3670016 | tf_op jit(solution)/shard_map/all_to_all | solution.py:90
  281.5 29.7 %all-to-all-done.1 = bf16[8,1,112,1024]{3,2,1,0:T(8,128)(2,1)S(1)} async-done(((bf16[8,1,112,1024]{3,2,1,0:T(8,128)(2,1)}), bf16[8,1,112,1024]{3,2,1,0:T(8,128)(2,1)S(1)}, u32[]{:S(2)}, u32[]{:S(2)}) %all-to-all-start.1) | async-done | bytes 1835040 | tf_op jit(solution)/shard_map/all_to_all | solution.py:90
  311.2 1.9 gather_fusion.1
  313.0 3.0 broadcast_select_fusion
  (27 shorter events, 0.9 us)
Async XLA Ops:
  5.1 56.9 %all-to-all-start = ((bf16[8,112,1024]{2,1,0:T(8,128)(2,1)}), bf16[8,112,1024]{2,1,0:T(8,128)(2,1)S(1)}, u32[]{:S(2)}, u32[]{:S(2)}) async-start(bf16[8,112,1024]{2,1,0:T(8,128)(2,1)} %bitcast.97), calls=%async_computation | async-start | bytes 3670016 | tf_op jit(solution)/shard_map/all_to_all | solution.py:76
  62.4 2.4 copy-start.1
  64.8 1.3 copy-start
  66.3 24.5 %collective-permute-start = (bf16[512,1024]{1,0:T(8,128)(2,1)S(1)}, bf16[512,1024]{1,0:T(8,128)(2,1)S(1)}, u32[]{:S(2)}, u32[]{:S(2)}) collective-permute-start(bf16[512,1024]{1,0:T(8,128)(2,1)S(1)} %dynamic-slice_bitcast_fusion.2), channel_id=1, source_target_pairs={{0,1},{1,0},{2,3},{3,2},{4,5},{5,4},{6,7},{7,6},{8,9},{9,8},{10,11... | collective-permute-start | bytes 3145736 | tf_op jit(solution)/shard_map/ppermute | solution.py:24
  92.4 13.2 %collective-permute-start.1 = (bf16[256,1024]{1,0:T(8,128)(2,1)S(1)}, bf16[256,1024]{1,0:T(8,128)(2,1)S(1)}, u32[]{:S(2)}, u32[]{:S(2)}) collective-permute-start(bf16[256,1024]{1,0:T(8,128)(2,1)S(1)} %fusion.13), channel_id=1, source_target_pairs={{0,2},{1,3},{2,0},{3,1},{4,6},{5,7},{6,4},{7,5},{8,10},{9,11},{10,... | collective-permute-start | bytes 1572872 | tf_op jit(solution)/shard_map/ppermute | solution.py:24
  105.8 9.2 %collective-permute-start.2 = (bf16[256,1024]{1,0:T(8,128)(2,1)S(1)}, bf16[256,1024]{1,0:T(8,128)(2,1)S(1)}, u32[]{:S(2)}, u32[]{:S(2)}) collective-permute-start(bf16[256,1024]{1,0:T(8,128)(2,1)S(1)} %fusion.12), channel_id=1, source_target_pairs={{0,2},{1,3},{2,0},{3,1},{4,6},{5,7},{6,4},{7,5},{8,10},{9,11},{10,... | collective-permute-start | bytes 1572872 | tf_op jit(solution)/shard_map/ppermute | solution.py:24
  115.2 20.3 %collective-permute-start.3 = (bf16[512,1024]{1,0:T(8,128)(2,1)S(1)}, bf16[512,1024]{1,0:T(8,128)(2,1)S(1)}, u32[]{:S(2)}, u32[]{:S(2)}) collective-permute-start(bf16[512,1024]{1,0:T(8,128)(2,1)S(1)} %pad_maximum_fusion), channel_id=1, source_target_pairs={{0,1},{1,0},{2,3},{3,2},{4,5},{5,4},{6,7},{7,6},{8,9},{9,8},{10,11... | collective-permute-start | bytes 3145736 | tf_op jit(solution)/shard_map/ppermute | solution.py:24
  136.1 2.5 copy-start.2
  143.1 19.4 %collective-permute-start.4 = (bf16[512,1024]{1,0:T(8,128)(2,1)S(1)}, bf16[512,1024]{1,0:T(8,128)(2,1)S(1)}, u32[]{:S(2)}, u32[]{:S(2)}) collective-permute-start(bf16[512,1024]{1,0:T(8,128)(2,1)S(1)} %dynamic-slice_bitcast_fusion.1), channel_id=1, source_target_pairs={{0,1},{1,0},{2,3},{3,2},{4,5},{5,4},{6,7},{7,6},{8,9},{9,8},{10,11... | collective-permute-start | bytes 3145736 | tf_op jit(solution)/shard_map/ppermute | solution.py:24
  163.0 14.2 %collective-permute-start.5 = (bf16[256,1024]{1,0:T(8,128)(2,1)S(1)}, bf16[256,1024]{1,0:T(8,128)(2,1)S(1)}, u32[]{:S(2)}, u32[]{:S(2)}) collective-permute-start(bf16[256,1024]{1,0:T(8,128)(2,1)S(1)} %fusion.14), channel_id=1, source_target_pairs={{0,2},{1,3},{2,0},{3,1},{4,6},{5,7},{6,4},{7,5},{8,10},{9,11},{10,... | collective-permute-start | bytes 1572872 | tf_op jit(solution)/shard_map/ppermute | solution.py:24
  177.3 9.2 %collective-permute-start.6 = (bf16[256,1024]{1,0:T(8,128)(2,1)S(1)}, bf16[256,1024]{1,0:T(8,128)(2,1)S(1)}, u32[]{:S(2)}, u32[]{:S(2)}) collective-permute-start(bf16[256,1024]{1,0:T(8,128)(2,1)S(1)} %fusion.11), channel_id=1, source_target_pairs={{0,2},{1,3},{2,0},{3,1},{4,6},{5,7},{6,4},{7,5},{8,10},{9,11},{10,... | collective-permute-start | bytes 1572872 | tf_op jit(solution)/shard_map/ppermute | solution.py:24
  186.7 16.2 %collective-permute-start.7 = (bf16[512,1024]{1,0:T(8,128)(2,1)S(1)}, bf16[512,1024]{1,0:T(8,128)(2,1)S(1)}, u32[]{:S(2)}, u32[]{:S(2)}) collective-permute-start(bf16[512,1024]{1,0:T(8,128)(2,1)S(1)} %pad_maximum_fusion.1), channel_id=1, source_target_pairs={{0,1},{1,0},{2,3},{3,2},{4,5},{5,4},{6,7},{7,6},{8,9},{9,8},{10,11... | collective-permute-start | bytes 3145736 | tf_op jit(solution)/shard_map/ppermute | solution.py:24
  208.3 2.4 copy-start.4
  210.8 15.4 %collective-permute-start.8 = (bf16[512,1024]{1,0:T(8,128)(2,1)S(1)}, bf16[512,1024]{1,0:T(8,128)(2,1)S(1)}, u32[]{:S(2)}, u32[]{:S(2)}) collective-permute-start(bf16[512,1024]{1,0:T(8,128)(2,1)S(1)} %dynamic-slice_bitcast_fusion), channel_id=1, source_target_pairs={{0,1},{1,0},{2,3},{3,2},{4,5},{5,4},{6,7},{7,6},{8,9},{9,8},{10,11... | collective-permute-start | bytes 3145736 | tf_op jit(solution)/shard_map/ppermute | solution.py:24
  226.7 11.9 %collective-permute-start.9 = (bf16[256,1024]{1,0:T(8,128)(2,1)S(1)}, bf16[256,1024]{1,0:T(8,128)(2,1)S(1)}, u32[]{:S(2)}, u32[]{:S(2)}) collective-permute-start(bf16[256,1024]{1,0:T(8,128)(2,1)S(1)} %fusion.15), channel_id=1, source_target_pairs={{0,2},{1,3},{2,0},{3,1},{4,6},{5,7},{6,4},{7,5},{8,10},{9,11},{10,... | collective-permute-start | bytes 1572872 | tf_op jit(solution)/shard_map/ppermute | solution.py:24
  238.7 9.2 %collective-permute-start.10 = (bf16[256,1024]{1,0:T(8,128)(2,1)S(1)}, bf16[256,1024]{1,0:T(8,128)(2,1)S(1)}, u32[]{:S(2)}, u32[]{:S(2)}) collective-permute-start(bf16[256,1024]{1,0:T(8,128)(2,1)S(1)} %fusion.10), channel_id=1, source_target_pairs={{0,2},{1,3},{2,0},{3,1},{4,6},{5,7},{6,4},{7,5},{8,10},{9,11},{10,... | collective-permute-start | bytes 1572872 | tf_op jit(solution)/shard_map/ppermute | solution.py:24
  248.1 14.9 %collective-permute-start.11 = (bf16[512,1024]{1,0:T(8,128)(2,1)S(1)}, bf16[512,1024]{1,0:T(8,128)(2,1)S(1)}, u32[]{:S(2)}, u32[]{:S(2)}) collective-permute-start(bf16[512,1024]{1,0:T(8,128)(2,1)S(1)} %pad_maximum_fusion.2), channel_id=1, source_target_pairs={{0,1},{1,0},{2,3},{3,2},{4,5},{5,4},{6,7},{7,6},{8,9},{9,8},{10,11... | collective-permute-start | bytes 3145736 | tf_op jit(solution)/shard_map/ppermute | solution.py:24
  277.1 4.3 %copy-start.3 = (s32[1,2]{1,0:T(1,128)S(1)}, s32[1,2]{1,0:T(1,128)}, u32[]{:S(2)}) copy-start(s32[1,2]{1,0:T(1,128)} %param.5) | copy-start | bytes 28
  277.8 33.3 %all-to-all-start.1 = ((bf16[8,1,112,1024]{3,2,1,0:T(8,128)(2,1)}), bf16[8,1,112,1024]{3,2,1,0:T(8,128)(2,1)S(1)}, u32[]{:S(2)}, u32[]{:S(2)}) async-start(bf16[8,1,112,1024]{3,2,1,0:T(8,128)(2,1)} %fusion.16), calls=%async_computation.1 | async-start | bytes 3670016 | tf_op jit(solution)/shard_map/all_to_all | solution.py:90
